TPU v7x, 32 devices: a whole 2x2x4 slice. The times are simulated.
32 devices in a mesh: tm: 1, space: 32 (over z, y, x, core).
Axes of the slice: x: 2, y: 2, z: 4, core: 2. Of those that a mesh axis runs over, the one named last changes fastest.
Arguments:
- links: float32 [8, 3, 2, 3, 2, 110592], P('tm', None, None, None, None, 'space'), may hold values from -1 to 1, as said below
Outputs:
- new_links: float32 [8, 3, 2, 3, 2, 110592], P('tm', None, None, None, None, 'space')
- theta: float32 [], replicated
- deficit: float32 [8], P('tm')
Inputs may be any that keep to these rules, and one draw needn't show every extreme that they name: `links`: each link's two stored rows are orthonormal complex 3-vectors, the first two rows of a special unitary matrix.
All inputs are finite; a program needn't handle non-finite values.
Results may differ from a plain program's by a relative error of at most 0.00013.
Values sent between devices are 32-bit elements; how exact they have to be, the bound alone decides.
A program may use at most 128 MiB of HBM per device.

v0:
```python
import math
import jax
import jax.numpy as jnp
from jax import lax
from jax.sharding import PartitionSpec as P

EXTENT = 48
root_three = math.sqrt(3.0)
step_size = 0.08
top_momentum = 12.0
storage_offset = 1


def from_behind(block, axis, distance):
    devices = range(lax.axis_size(axis))
    route = [((i - distance) % len(devices), i) for i in devices]
    return lax.ppermute(block, axis, route)


def complex_mul(p, q):
    return (p[0] * q[0] - p[1] * q[1], p[0] * q[1] + p[1] * q[0])


def complex_add(p, q):
    return (p[0] + q[0], p[1] + q[1])


def complex_sub(p, q):
    return (p[0] - q[0], p[1] - q[1])


def complex_conj(p):
    return (p[0], -p[1])


def matrix_mul(left, right):
    rows_out = []
    for i in range(len(left)):
        entries = []
        for j in range(3):
            summed = complex_mul(left[i][0], right[0][j])
            for k in (1, 2):
                summed = complex_add(summed, complex_mul(left[i][k], right[k][j]))
            entries.append(summed)
        rows_out.append(entries)
    return rows_out


def dagger_of(matrix):
    return [[complex_conj(matrix[j][i]) for j in range(3)] for i in range(3)]


def cross_conj(row_one, row_two):
    row_three = []
    for k in range(3):
        a = complex_mul(row_one[(k + 1) % 3], row_two[(k + 2) % 3])
        b = complex_mul(row_one[(k + 2) % 3], row_two[(k + 1) % 3])
        row_three.append(complex_conj(complex_sub(a, b)))
    return row_three


def full_matrix(entry_of):
    row_one = [(entry_of(0, c, 0), entry_of(0, c, 1)) for c in range(3)]
    row_two = [(entry_of(1, c, 0), entry_of(1, c, 1)) for c in range(3)]
    return [row_one, row_two, cross_conj(row_one, row_two)]


def link_matrix(arr):
    return full_matrix(lambda r, c, p: arr[:, r, c, p])


def gradient_of(current, behind):
    gradient = []
    for i in range(3):
        entries = []
        for j in range(3):
            summed = complex_sub(behind[0][i][j], current[0][i][j])
            for d in (1, 2):
                summed = complex_add(summed, complex_sub(behind[d][i][j], current[d][i][j]))
            entries.append(summed)
        gradient.append(entries)
    return gradient


def algebra_of(gradient):
    return [
        gradient[0][1][1] + gradient[1][0][1],
        gradient[0][1][0] - gradient[1][0][0],
        gradient[0][0][1] - gradient[1][1][1],
        gradient[0][2][1] + gradient[2][0][1],
        gradient[0][2][0] - gradient[2][0][0],
        gradient[1][2][1] + gradient[2][1][1],
        gradient[1][2][0] - gradient[2][1][0],
        (gradient[0][0][1] + gradient[1][1][1] - 2.0 * gradient[2][2][1]) / root_three,
    ]


def rotation_of(algebra):
    half_step = 0.5 * step_size
    zeros_like = jnp.zeros_like(algebra[0])
    diag_zero = algebra[2] + algebra[7] / root_three
    diag_one = -algebra[2] + algebra[7] / root_three
    diag_two = -2.0 * algebra[7] / root_three
    hermitian = [
        [(diag_zero, zeros_like), (algebra[0], -algebra[1]), (algebra[3], -algebra[4])],
        [(algebra[0], algebra[1]), (diag_one, zeros_like), (algebra[5], -algebra[6])],
        [(algebra[3], algebra[4]), (algebra[5], algebra[6]), (diag_two, zeros_like)],
    ]
    generator = [[(-half_step * h[1], half_step * h[0]) for h in row] for row in hermitian]
    square = matrix_mul(generator[:2], generator)
    rows_two = []
    for i in range(2):
        entries = []
        for j in range(3):
            real_value = generator[i][j][0] + 0.5 * square[i][j][0]
            if i == j:
                real_value = real_value + 1.0
            entries.append((real_value, generator[i][j][1] + 0.5 * square[i][j][1]))
        rows_two.append(entries)
    length = jnp.sqrt(sum((p[0] * p[0] + p[1] * p[1] for p in rows_two[0])))
    row_one = [(p[0] / length, p[1] / length) for p in rows_two[0]]
    correlation = complex_mul(complex_conj(row_one[0]), rows_two[1][0])
    for k in (1, 2):
        correlation = complex_add(
            correlation, complex_mul(complex_conj(row_one[k]), rows_two[1][k])
        )
    row_two = [complex_sub(rows_two[1][k], complex_mul(correlation, row_one[k])) for k in range(3)]
    length = jnp.sqrt(sum((p[0] * p[0] + p[1] * p[1] for p in row_two)))
    row_two = [(p[0] / length, p[1] / length) for p in row_two]
    return [row_one, row_two, cross_conj(row_one, row_two)]


def two_rows(product, axis):
    return jnp.stack(
        [
            jnp.stack([jnp.stack(product[r][c], axis=axis) for c in range(3)], axis=axis)
            for r in range(2)
        ],
        axis=axis,
    )


def matrix_stack(matrix):
    return jnp.stack([jnp.stack([jnp.stack(matrix[i][j]) for j in range(3)]) for i in range(3)])


def matrix_from(stacked):
    return [[(stacked[i, j, 0], stacked[i, j, 1]) for j in range(3)] for i in range(3)]


def plane_step(values, einsum_form, cosine_table, sine_table, sign_value, pair_count):
    highest = lax.Precision.HIGHEST
    with_cos = jnp.einsum(einsum_form, values, cosine_table, precision=highest)
    with_sin = jnp.einsum(einsum_form, values, sine_table, precision=highest)
    dims_shape = with_cos.shape
    with_cos = with_cos.reshape(dims_shape[0], dims_shape[1], pair_count, 2, -1)
    with_sin = with_sin.reshape(dims_shape[0], dims_shape[1], pair_count, 2, -1)
    real_out = with_cos[:, :, :, 0] - sign_value * with_sin[:, :, :, 1]
    imag_out = with_cos[:, :, :, 1] + sign_value * with_sin[:, :, :, 0]
    return jnp.stack([real_out, imag_out], axis=3).reshape(dims_shape)


def body(links):
    highest = lax.Precision.HIGHEST
    extent = EXTENT
    slices = links.shape[0]
    local_sites = links.shape[-1]
    plane_size = extent * extent
    lower_width = (extent - 1) * extent
    rows_dev = local_sites // extent
    device = lax.axis_index("space")
    site_index = jnp.arange(local_sites, dtype=jnp.int32)
    xcoord = site_index % extent
    zcoord = (device * rows_dev + site_index // extent - storage_offset) % extent
    along_x = links[:, 0]
    along_y = links[:, 1]
    along_z = links[:, 2]
    below_piece = jnp.concatenate(
        [along_y[..., local_sites - plane_size :], along_z[..., local_sites - extent :]], axis=-1
    )
    from_below = from_behind(below_piece, "space", 1)
    from_above = from_behind(along_z[..., : plane_size - extent], "space", -1)
    behind_x = jnp.where(
        xcoord == 0, jnp.roll(along_x, -(extent - 1), axis=-1), jnp.roll(along_x, 1, axis=-1)
    )
    behind_y = jnp.concatenate(
        [from_below[..., :plane_size], along_y[..., : local_sites - plane_size]], axis=-1
    )
    near_z = jnp.concatenate(
        [from_below[..., plane_size:], along_z[..., : local_sites - extent]], axis=-1
    )
    wrap_z = jnp.concatenate([along_z[..., plane_size - extent :], from_above], axis=-1)
    behind_z = jnp.where(zcoord == 0, wrap_z, near_z)
    current = [link_matrix(along_x), link_matrix(along_y), link_matrix(along_z)]
    behind = [link_matrix(behind_x), link_matrix(behind_y), link_matrix(behind_z)]
    algebra = algebra_of(gradient_of(current, behind))
    theta_part = sum((jnp.sum(a * a) for a in algebra))
    theta_total = lax.psum(theta_part, ("tm", "space"))
    wave_number = jnp.arange(extent, dtype=jnp.int32)
    angle_table = (
        2.0
        * math.pi
        / extent
        * (wave_number[:, None] * wave_number[None, :] % extent).astype(jnp.float32)
    )
    cosine_table = jnp.cos(angle_table)
    sine_table = jnp.sin(angle_table)
    fields = jnp.stack(algebra).reshape(8, slices, rows_dev, extent)
    paired = fields.reshape(4, 2, slices, rows_dev, extent)
    even_part = paired[:, 0]
    odd_part = paired[:, 1]
    real_x = jnp.einsum("csqx,kx->qcks", even_part, cosine_table, precision=highest)
    real_x = real_x + jnp.einsum("csqx,kx->qcks", odd_part, sine_table, precision=highest)
    imag_x = jnp.einsum("csqx,kx->qcks", odd_part, cosine_table, precision=highest)
    imag_x = imag_x - jnp.einsum("csqx,kx->qcks", even_part, sine_table, precision=highest)
    packed = jnp.stack([real_x, imag_x], axis=3).reshape(rows_dev, 4 * extent * 2 * slices)
    planes = lax.all_to_all(packed, "space", split_axis=1, concat_axis=0, tiled=True)
    pair_count = planes.shape[1] // (2 * slices)
    planes = jnp.roll(planes, -storage_offset, axis=0)
    planes = planes.reshape(extent, extent, planes.shape[1])
    planes = plane_step(planes, "yzc,kz->ykc", cosine_table, sine_table, -1.0, pair_count)
    planes = plane_step(planes, "yzc,ky->kzc", cosine_table, sine_table, -1.0, pair_count)
    pair_kx = (device * pair_count + jnp.arange(pair_count, dtype=jnp.int32)) % extent
    wave_term = 4.0 * jnp.sin(math.pi * wave_number.astype(jnp.float32) / extent) ** 2
    wave_pair = 4.0 * jnp.sin(math.pi * pair_kx.astype(jnp.float32) / extent) ** 2
    momentum = wave_term[:, None, None] + wave_term[None, :, None] + wave_pair[None, None, :]
    zero_mode = (
        wave_number[:, None, None] + wave_number[None, :, None] + pair_kx[None, None, :] == 0
    )
    factor = jnp.where(
        zero_mode, 0.0, top_momentum / (extent**3 * jnp.where(zero_mode, 1.0, momentum))
    )
    planes = (
        planes.reshape(extent, extent, pair_count, 2 * slices) * factor[:, :, :, None]
    ).reshape(extent, extent, -1)
    planes = plane_step(planes, "yzc,kz->ykc", cosine_table, sine_table, 1.0, pair_count)
    planes = plane_step(planes, "yzc,ky->kzc", cosine_table, sine_table, 1.0, pair_count)
    planes = jnp.roll(planes.reshape(plane_size, -1), storage_offset, axis=0)
    returned = lax.all_to_all(planes, "space", split_axis=0, concat_axis=1, tiled=True)
    returned = returned.reshape(rows_dev, 4, extent, 2, slices)
    real_back = returned[:, :, :, 0]
    imag_back = returned[:, :, :, 1]
    even_smooth = jnp.einsum("qcks,kx->csqx", real_back, cosine_table, precision=highest)
    even_smooth = even_smooth - jnp.einsum(
        "qcks,kx->csqx", imag_back, sine_table, precision=highest
    )
    odd_smooth = jnp.einsum("qcks,kx->csqx", real_back, sine_table, precision=highest)
    odd_smooth = odd_smooth + jnp.einsum(
        "qcks,kx->csqx", imag_back, cosine_table, precision=highest
    )
    smooth = jnp.stack([even_smooth, odd_smooth], axis=1).reshape(8, slices, local_sites)
    rotation = rotation_of([smooth[a] for a in range(8)])
    stacked = matrix_stack(rotation)
    upper_rim = from_behind(stacked[..., :plane_size], "space", -1)
    lower_rim = from_behind(stacked[..., local_sites - lower_width :], "space", 1)
    wide_rot = matrix_from(jnp.concatenate([lower_rim, stacked, upper_rim], axis=-1))
    ahead_x = jax.tree.map(
        lambda a: jnp.where(
            xcoord == extent - 1, jnp.roll(a, extent - 1, axis=-1), jnp.roll(a, -1, axis=-1)
        ),
        rotation,
    )
    ahead_y = jax.tree.map(
        lambda a: a[..., lower_width + plane_size : lower_width + plane_size + local_sites],
        wide_rot,
    )
    ahead_z = jax.tree.map(
        lambda a: jnp.where(
            zcoord == extent - 1,
            a[..., :local_sites],
            a[..., lower_width + extent : lower_width + extent + local_sites],
        ),
        wide_rot,
    )
    ahead_all = [ahead_x, ahead_y, ahead_z]
    new_dirs = []
    deficit_part = jnp.zeros((slices,), jnp.float32)
    for d in range(3):
        product = matrix_mul(matrix_mul(rotation, current[d]), dagger_of(ahead_all[d]))
        deficit_part = deficit_part + jnp.sum(
            3.0 - product[0][0][0] - product[1][1][0] - product[2][2][0], axis=-1
        )
        new_dirs.append(two_rows(product, 1))
    new_links = jnp.stack(new_dirs, axis=1)
    deficit_total = lax.psum(deficit_part, "space")
    theta = theta_total / (slices * lax.axis_size("tm") * extent**3)
    deficit = deficit_total / extent**3
    return (new_links, theta, deficit)


def solution(mesh):
    placed = (P("tm", None, None, None, None, "space"),)
    return jax.shard_map(
        body,
        mesh=mesh,
        in_specs=placed,
        out_specs=(P("tm", None, None, None, None, "space"), P(), P("tm")),
        check_vma=False,
    )
```

profile of v0, /device:TPU:12, one launch (start us, length us, event | category | flops | bytes accessed | tf_op | source)
XLA Modules:
  0.0 409.1 jit_solution(4929725969459849419)
XLA Ops:
  0.6 3.5 fusion.979
  12.0 16.0 %collective-permute-done = f32[8,2,3,2,2352]{4,0,3,2,1:T(8,128)} collective-permute-done((f32[8,2,3,2,2352]{4,0,3,2,1:T(8,128)}, f32[8,2,3,2,2352]{4,0,3,2,1:T(8,128)}, u32[]{:S(2)}, u32[]{:S(2)}) %collective-permute-start) | collective-permute-done | bytes 903200 | tf_op jit(solution)/shard_map/ppermute | solution.py:17
  40.9 3.7 reshape_reshape.9
  44.6 4.7 %fusion.9 = f32[48,4,8,72]{3,0,2,1:T(8,128)S(1)} fusion(f32[4,2,8,72,48]{4,3,2,1,0:T(8,128)} %reshape_reshape.9), kind=kOutput, calls=%fused_computation.67 | convolution fusion | flops 63721728 | bytes 1622016 | tf_op jit(solution)/shard_map/csqx,kx->qcks/dot_general | solution.py:214
  49.3 4.6 %fusion.8 = f32[48,4,8,72]{3,0,2,1:T(8,128)S(1)} fusion(f32[4,2,8,72,48]{4,3,2,1,0:T(8,128)} %reshape_reshape.9), kind=kOutput, calls=%fused_computation.66 | convolution fusion | flops 63721728 | bytes 1622016 | tf_op jit(solution)/shard_map/csqx,kx->qcks/dot_general | solution.py:212
  53.9 3.3 fusion.2
  57.3 3.3 fusion.3
  62.3 2.9 copy.286
  65.3 6.8 %all-to-all-start = ((f32[72,32,96]{2,0,1:T(8,128)}), f32[72,32,96]{2,0,1:T(8,128)}, u32[]{:S(2)}, u32[]{:S(2)}) async-start(f32[72,32,96]{2,0,1:T(8,128)} %copy.286), calls=%async_computation | async-start | bytes 2359296 | tf_op jit(solution)/shard_map/all_to_all | solution.py:217
  74.0 2.8 copy.300
  76.8 22.8 %all-to-all-done = f32[72,32,96]{2,0,1:T(8,128)} async-done(((f32[72,32,96]{2,0,1:T(8,128)}), f32[72,32,96]{2,0,1:T(8,128)}, u32[]{:S(2)}, u32[]{:S(2)}) %all-to-all-start) | async-done | bytes 884768 | tf_op jit(solution)/shard_map/all_to_all | solution.py:217
  101.8 2.3 convolution_bitcast_fusion.2
  104.1 2.3 convolution_bitcast_fusion.3
  106.4 2.9 copy.357
  109.2 2.9 copy.355
  112.1 2.6 fusion.7
  116.4 3.1 copy.295
  119.5 10.3 %fusion.728 = f32[48,48,6,2,8]{1,0,4,3,2:T(8,128)S(1)} fusion(f32[48,6,2,8,48]{4,0,3,2,1:T(8,128)} %bitcast.4454), kind=kOutput, calls=%fused_computation.1642 | convolution fusion | flops 127422720 | bytes 1769472 | tf_op jit(solution)/shard_map/yzc,ky->kzc/dot_general | solution.py:154
  129.8 8.5 %fusion.738 = f32[48,48,6,2,8]{1,0,4,3,2:T(8,128)S(1)} fusion(f32[48,6,2,8,48]{4,0,3,2,1:T(8,128)S(1)} %bitcast.4455), kind=kOutput, calls=%fused_computation.1652 | convolution fusion | flops 127422720 | bytes 1769472 | tf_op jit(solution)/shard_map/yzc,ky->kzc/dot_general | solution.py:153
  140.2 3.2 copy.299
  143.4 4.1 convolution_bitcast_fusion
  147.5 2.3 convolution_bitcast_fusion.1
  149.8 2.8 copy.304
  152.6 2.9 copy.302
  155.6 2.6 slice_subtract_fusion.1
  159.8 3.2 copy.305
  163.0 10.3 %fusion.726 = f32[48,48,6,2,8]{1,0,4,3,2:T(8,128)S(1)} fusion(f32[48,6,2,8,48]{4,0,3,2,1:T(8,128)} %bitcast.4456), kind=kOutput, calls=%fused_computation.1640 | convolution fusion | flops 127422720 | bytes 1769472 | tf_op jit(solution)/shard_map/yzc,ky->kzc/dot_general | solution.py:154
  173.4 8.5 %fusion.740 = f32[48,48,6,2,8]{1,0,4,3,2:T(8,128)S(1)} fusion(f32[48,6,2,8,48]{4,0,3,2,1:T(8,128)S(1)} %bitcast.4457), kind=kOutput, calls=%fused_computation.1654 | convolution fusion | flops 127422720 | bytes 1769472 | tf_op jit(solution)/shard_map/yzc,ky->kzc/dot_general | solution.py:153
  183.7 2.4 reshape_reshape.11
  189.1 2.4 pad_maximum_fusion.9
  191.6 5.0 %all-to-all-start.1 = ((f32[32,72,96]{2,1,0:T(8,128)}), f32[32,72,96]{2,1,0:T(8,128)}, u32[]{:S(2)}, u32[]{:S(2)}) async-start(f32[32,72,96]{2,1,0:T(8,128)} %bitcast.4470), calls=%async_computation.1 | async-start | bytes 2359296 | tf_op jit(solution)/shard_map/all_to_all | solution.py:239
  198.5 25.8 %all-to-all-done.1 = f32[32,72,96]{2,1,0:T(8,128)} async-done(((f32[32,72,96]{2,1,0:T(8,128)}), f32[32,72,96]{2,1,0:T(8,128)}, u32[]{:S(2)}, u32[]{:S(2)}) %all-to-all-start.1) | async-done | bytes 884768 | tf_op jit(solution)/shard_map/all_to_all | solution.py:239
  224.3 2.9 copy.310
  233.7 2.9 copy.313
  252.0 2.6 collective-permute-start.3
  258.4 25.5 %collective-permute-done.2 = f32[3,3,2,8,2256]{4,3,2,1,0:T(8,128)} collective-permute-done((f32[3,3,2,8,2256]{4,3,2,1,0:T(8,128)S(1)}, f32[3,3,2,8,2256]{4,3,2,1,0:T(8,128)}, u32[]{:S(2)}, u32[]{:S(2)}) %collective-permute-start.2) | collective-permute-done | bytes 1299488 | tf_op jit(solution)/shard_map/ppermute | solution.py:17
  283.9 6.6 %concatenate.1157 = f32[3,3,2,8,8016]{4,3,2,1,0:T(8,128)} concatenate(f32[3,3,2,8,2256]{4,3,2,1,0:T(8,128)} %collective-permute-done.2, f32[3,3,2,8,3456]{4,3,2,1,0:T(8,128)} %copy-done.7, f32[3,3,2,8,2304]{4,3,2,1,0:T(8,128)} %collective-permute-done.3), dimensions={4} | concatenate | bytes 9234432 | tf_op jit(solution)/shard_map/concatenate | solution.py:256
  290.7 2.9 slice_bitcast_fusion.17
  293.8 2.9 fusion.706
  328.6 2.8 fusion.707
  341.3 2.5 fusion.170
  344.3 2.5 fusion.177
  347.4 2.6 fusion.95
  350.6 2.4 fusion.102
  354.5 2.7 pad_maximum_fusion
  357.7 3.4 fusion.708
  361.7 4.0 copy.332
  365.7 40.9 %all-reduce = (f32[]{:T(128)}, f32[8]{0:T(128)S(1)}) all-reduce(f32[]{:T(128)S(6)} %add.9190, f32[8]{0:T(128)S(1)} %add_add_fusion.11), channel_id=1, replica_groups=mesh['tm'=1,'space'=32] {'tm','space'}, use_global_device_ids=true, to_apply=%region_8.9 | all-reduce | flops 9 | bytes 72 | tf_op jit(solution)/shard_map/psum | solution.py:198
  (442 shorter events, 104.5 us)
Async XLA Ops:
  5.2 24.8 %collective-permute-start.1 = (f32[8,2,3,2,2256]{4,0,3,2,1:T(8,128)}, f32[8,2,3,2,2256]{4,0,3,2,1:T(8,128)}, u32[]{:S(2)}, u32[]{:S(2)}) collective-permute-start(f32[8,2,3,2,2256]{4,0,3,2,1:T(8,128)} %slice.1086), channel_id=1, source_target_pairs={{1,0},{2,1},{3,2},{4,3},{5,4},{6,5},{7,6},{8,7},{9,8},{10,9},{11,1... | collective-permute-start | bytes 2598920 | tf_op jit(solution)/shard_map/ppermute | solution.py:17
  6.3 3.9 copy-start.4
  7.5 20.5 %collective-permute-start = (f32[8,2,3,2,2352]{4,0,3,2,1:T(8,128)}, f32[8,2,3,2,2352]{4,0,3,2,1:T(8,128)}, u32[]{:S(2)}, u32[]{:S(2)}) collective-permute-start(f32[8,2,3,2,2352]{4,0,3,2,1:T(8,128)} %pad_maximum_fusion.10), channel_id=1, source_target_pairs={{31,0},{0,1},{1,2},{2,3},{3,4},{4,5},{5,6},{6,7},{7,8},{8,9},{9,10... | collective-permute-start | bytes 2709512 | tf_op jit(solution)/shard_map/ppermute | solution.py:17
  12.0 27.8 %copy-start = (f32[8,2,3,2,3456]{4,0,3,2,1:T(8,128)}, f32[8,2,3,2,3456]{4,0,3,2,1:T(8,128)S(1)}, u32[]{:S(2)}) copy-start(f32[8,2,3,2,3456]{4,0,3,2,1:T(8,128)S(1)} %maximum_select_fusion) | copy-start | bytes 3981316
  12.0 18.1 %copy-start.91 = (f32[8,2,3,2,1200]{4,0,3,2,1:T(8,128)S(1)}, f32[8,2,3,2,1200]{4,0,3,2,1:T(8,128)}, u32[]{:S(2)}) copy-start(f32[8,2,3,2,1200]{4,0,3,2,1:T(8,128)} %slice.1085) | copy-start | bytes 1382404
  32.0 7.8 %copy-start.2 = (f32[8,2,3,2,3456]{4,0,3,2,1:T(8,128)}, f32[8,2,3,2,3456]{4,0,3,2,1:T(8,128)S(1)}, u32[]{:S(2)}) copy-start(f32[8,2,3,2,3456]{4,0,3,2,1:T(8,128)S(1)} %maximum_select_fusion.1) | copy-start | bytes 3981316
  32.9 7.0 %copy-start.13 = (f32[8,1,1,1,3456]{4,0,3,2,1:T(8,128)}, f32[8,1,1,1,3456]{4,0,3,2,1:T(8,128)S(1)}, u32[]{:S(2)}) copy-start(f32[8,1,1,1,3456]{4,0,3,2,1:T(8,128)S(1)} %get-tuple-element.94) | copy-start | bytes 331780
  32.9 7.0 %copy-start.17 = (f32[8,1,1,1,3456]{4,0,3,2,1:T(8,128)}, f32[8,1,1,1,3456]{4,0,3,2,1:T(8,128)S(1)}, u32[]{:S(2)}) copy-start(f32[8,1,1,1,3456]{4,0,3,2,1:T(8,128)S(1)} %get-tuple-element.93) | copy-start | bytes 331780
  33.5 6.3 %copy-start.15 = (f32[8,1,1,1,3456]{4,0,3,2,1:T(8,128)}, f32[8,1,1,1,3456]{4,0,3,2,1:T(8,128)S(1)}, u32[]{:S(2)}) copy-start(f32[8,1,1,1,3456]{4,0,3,2,1:T(8,128)S(1)} %get-tuple-element.91) | copy-start | bytes 331780
  33.5 6.3 %copy-start.19 = (f32[8,1,1,1,3456]{4,0,3,2,1:T(8,128)}, f32[8,1,1,1,3456]{4,0,3,2,1:T(8,128)S(1)}, u32[]{:S(2)}) copy-start(f32[8,1,1,1,3456]{4,0,3,2,1:T(8,128)S(1)} %get-tuple-element.90) | copy-start | bytes 331780
  35.8 4.1 copy-start.47
  35.8 4.1 %copy-start.50 = (f32[8,1,1,1,3456]{4,0,3,2,1:T(8,128)}, f32[8,1,1,1,3456]{4,0,3,2,1:T(8,128)S(1)}, u32[]{:S(2)}) copy-start(f32[8,1,1,1,3456]{4,0,3,2,1:T(8,128)S(1)} %get-tuple-element.230) | copy-start | bytes 331780
  36.8 3.1 copy-start.55
  44.6 9.3 %copy-start.10 = (f32[4,2,8,72,48]{4,3,2,1,0:T(8,128)S(1)}, f32[4,2,8,72,48]{4,3,2,1,0:T(8,128)}, u32[]{:S(2)}) copy-start(f32[4,2,8,72,48]{4,3,2,1,0:T(8,128)} %reshape_reshape.9) | copy-start | bytes 2654212
  65.3 34.4 %all-to-all-start = ((f32[72,32,96]{2,0,1:T(8,128)}), f32[72,32,96]{2,0,1:T(8,128)}, u32[]{:S(2)}, u32[]{:S(2)}) async-start(f32[72,32,96]{2,0,1:T(8,128)} %copy.286), calls=%async_computation | async-start | bytes 2359296 | tf_op jit(solution)/shard_map/all_to_all | solution.py:217
  119.5 10.3 %copy-start.8 = (f32[48,48,96]{0,1,2:T(8,128)S(1)}, f32[48,48,96]{0,1,2:T(8,128)}, u32[]{:S(2)}) copy-start(f32[48,48,96]{0,1,2:T(8,128)} %copy.295) | copy-start | bytes 2654212
  143.4 4.1 copy-start.11
  143.4 4.1 copy-start.12
  163.0 10.3 %copy-start.9 = (f32[48,96,48]{2,0,1:T(8,128)S(1)}, f32[48,96,48]{2,0,1:T(8,128)}, u32[]{:S(2)}) copy-start(f32[48,96,48]{2,0,1:T(8,128)} %copy.305) | copy-start | bytes 2654212
  191.6 32.8 %all-to-all-start.1 = ((f32[32,72,96]{2,1,0:T(8,128)}), f32[32,72,96]{2,1,0:T(8,128)}, u32[]{:S(2)}, u32[]{:S(2)}) async-start(f32[32,72,96]{2,1,0:T(8,128)} %bitcast.4470), calls=%async_computation.1 | async-start | bytes 2359296 | tf_op jit(solution)/shard_map/all_to_all | solution.py:239
  243.0 14.2 %copy-start.29 = (f32[8,3456]{1,0:T(8,128)}, f32[8,3456]{1,0:T(8,128)S(1)}, u32[]{:S(2)}) copy-start(f32[8,3456]{1,0:T(8,128)S(1)} %get-tuple-element.199) | copy-start | bytes 331780
  243.1 14.2 %copy-start.32 = (f32[8,3456]{1,0:T(8,128)}, f32[8,3456]{1,0:T(8,128)S(1)}, u32[]{:S(2)}) copy-start(f32[8,3456]{1,0:T(8,128)S(1)} %get-tuple-element.200) | copy-start | bytes 331780
  243.1 14.2 %copy-start.35 = (f32[8,3456]{1,0:T(8,128)}, f32[8,3456]{1,0:T(8,128)S(1)}, u32[]{:S(2)}) copy-start(f32[8,3456]{1,0:T(8,128)S(1)} %get-tuple-element.201) | copy-start | bytes 331780
  243.1 14.2 %copy-start.38 = (f32[8,3456]{1,0:T(8,128)}, f32[8,3456]{1,0:T(8,128)S(1)}, u32[]{:S(2)}) copy-start(f32[8,3456]{1,0:T(8,128)S(1)} %get-tuple-element.203) | copy-start | bytes 331780
  243.1 14.2 %copy-start.41 = (f32[8,3456]{1,0:T(8,128)}, f32[8,3456]{1,0:T(8,128)S(1)}, u32[]{:S(2)}) copy-start(f32[8,3456]{1,0:T(8,128)S(1)} %get-tuple-element.205) | copy-start | bytes 331780
  243.1 14.2 %copy-start.44 = (f32[8,3456]{1,0:T(8,128)}, f32[8,3456]{1,0:T(8,128)S(1)}, u32[]{:S(2)}) copy-start(f32[8,3456]{1,0:T(8,128)S(1)} %get-tuple-element.208) | copy-start | bytes 331780
  252.0 32.0 %collective-permute-start.2 = (f32[3,3,2,8,2256]{4,3,2,1,0:T(8,128)S(1)}, f32[3,3,2,8,2256]{4,3,2,1,0:T(8,128)}, u32[]{:S(2)}, u32[]{:S(2)}) collective-permute-start(f32[3,3,2,8,2256]{4,3,2,1,0:T(8,128)S(1)} %slice.1270), channel_id=1, source_target_pairs={{31,0},{0,1},{1,2},{2,3},{3,4},{4,5},{5,6},{6,7},{7,8},{8,9},{9,10... | collective-permute-start | bytes 3898376 | tf_op jit(solution)/shard_map/ppermute | solution.py:17
  252.0 31.9 %collective-permute-start.3 = (f32[3,3,2,8,2304]{4,3,2,1,0:T(8,128)S(1)}, f32[3,3,2,8,2304]{4,3,2,1,0:T(8,128)}, u32[]{:S(2)}, u32[]{:S(2)}) collective-permute-start(f32[3,3,2,8,2304]{4,3,2,1,0:T(8,128)S(1)} %slice.1271), channel_id=1, source_target_pairs={{1,0},{2,1},{3,2},{4,3},{5,4},{6,5},{7,6},{8,7},{9,8},{10,9},{11,1... | collective-permute-start | bytes 3981320 | tf_op jit(solution)/shard_map/ppermute | solution.py:17
  290.7 3.1 copy-start.123
  296.7 31.8 %copy-start.69 = (f32[8,3456]{1,0:T(8,128)}, f32[8,3456]{1,0:T(8,128)S(1)}, u32[]{:S(2)}) copy-start(f32[8,3456]{1,0:T(8,128)S(1)} %get-tuple-element.21) | copy-start | bytes 331780
  296.7 31.8 %copy-start.71 = (f32[8,3456]{1,0:T(8,128)}, f32[8,3456]{1,0:T(8,128)S(1)}, u32[]{:S(2)}) copy-start(f32[8,3456]{1,0:T(8,128)S(1)} %get-tuple-element.22) | copy-start | bytes 331780
  296.7 31.8 %copy-start.73 = (f32[8,3456]{1,0:T(8,128)}, f32[8,3456]{1,0:T(8,128)S(1)}, u32[]{:S(2)}) copy-start(f32[8,3456]{1,0:T(8,128)S(1)} %get-tuple-element.23) | copy-start | bytes 331780
  296.7 31.8 %copy-start.75 = (f32[8,3456]{1,0:T(8,128)}, f32[8,3456]{1,0:T(8,128)S(1)}, u32[]{:S(2)}) copy-start(f32[8,3456]{1,0:T(8,128)S(1)} %get-tuple-element.24) | copy-start | bytes 331780
  296.7 31.8 %copy-start.77 = (f32[8,3456]{1,0:T(8,128)}, f32[8,3456]{1,0:T(8,128)S(1)}, u32[]{:S(2)}) copy-start(f32[8,3456]{1,0:T(8,128)S(1)} %get-tuple-element.26) | copy-start | bytes 331780
  296.7 31.8 %copy-start.79 = (f32[8,3456]{1,0:T(8,128)}, f32[8,3456]{1,0:T(8,128)S(1)}, u32[]{:S(2)}) copy-start(f32[8,3456]{1,0:T(8,128)S(1)} %get-tuple-element.44) | copy-start | bytes 331780
  296.7 31.8 %copy-start.81 = (f32[8,3456]{1,0:T(8,128)}, f32[8,3456]{1,0:T(8,128)S(1)}, u32[]{:S(2)}) copy-start(f32[8,3456]{1,0:T(8,128)S(1)} %get-tuple-element.45) | copy-start | bytes 331780
  296.7 31.8 %copy-start.83 = (f32[8,3456]{1,0:T(8,128)}, f32[8,3456]{1,0:T(8,128)S(1)}, u32[]{:S(2)}) copy-start(f32[8,3456]{1,0:T(8,128)S(1)} %get-tuple-element.46) | copy-start | bytes 331780
  296.7 31.8 %copy-start.85 = (f32[8,3456]{1,0:T(8,128)}, f32[8,3456]{1,0:T(8,128)S(1)}, u32[]{:S(2)}) copy-start(f32[8,3456]{1,0:T(8,128)S(1)} %get-tuple-element.47) | copy-start | bytes 331780
  296.7 31.8 %copy-start.87 = (f32[8,3456]{1,0:T(8,128)}, f32[8,3456]{1,0:T(8,128)S(1)}, u32[]{:S(2)}) copy-start(f32[8,3456]{1,0:T(8,128)S(1)} %get-tuple-element.48) | copy-start | bytes 331780
  296.7 31.8 %copy-start.89 = (f32[8,3456]{1,0:T(8,128)}, f32[8,3456]{1,0:T(8,128)S(1)}, u32[]{:S(2)}) copy-start(f32[8,3456]{1,0:T(8,128)S(1)} %get-tuple-element.49) | copy-start | bytes 331780
  296.8 31.8 %copy-start.92 = (f32[8,3456]{1,0:T(8,128)}, f32[8,3456]{1,0:T(8,128)S(1)}, u32[]{:S(2)}) copy-start(f32[8,3456]{1,0:T(8,128)S(1)} %get-tuple-element.25) | copy-start | bytes 331780
  318.4 10.1 %copy-start.124 = (pred[3456]{0:T(1024)(128)(4,1)S(1)}, pred[3456]{0:T(1024)(128)(4,1)}, u32[]{:S(2)}) copy-start(pred[3456]{0:T(1024)(128)(4,1)} %broadcast_compare_fusion) | copy-start | bytes 10372
  347.4 3.2 copy-start.49
  347.4 3.2 copy-start.54
  354.5 3.1 copy-start.113
  354.5 3.1 copy-start.114
  354.5 3.2 copy-start.115
  354.5 3.2 copy-start.116
  (83 other events, 207.1 us)
where the time goes:
time: 415 us; the launch traced here: 409 us
  local copies, waits for them, and re-layouts  116 us (28%)
  waiting for transfers between devices  90.2 us (22%)
  other arithmetic  69.1 us (17%)
  matrix products  68.1 us (16%)
  blocking collectives  40.9 us (10%)
  starting transfers between devices  15.4 us (4%)
  between operations  9.56 us (2%)
    ppermute x4, waiting for transfers between devices, from_behind(): return lax.ppermute(block, axis, route)  41.5 us
    psum x1, blocking collectives, body(): theta_total = lax.psum(theta_part, ('tm', 'space'))  40.9 us
    dot_general x4, matrix products, plane_step(): with_sin = jnp.einsum(einsum_form, values, sine_table, precision=highest)  26.9 us
    all_to_all x1, waiting for transfers between devices, body(): lax.all_to_all(planes, 'space', split_axis=0, concat_axis=1, tiled=True)  25.8 us
    all_to_all x1, waiting for transfers between devices, body(): lax.all_to_all(packed, 'space', split_axis=1, concat_axis=0, tiled=True)  22.8 us
    dot_general x4, matrix products, plane_step(): with_cos = jnp.einsum(einsum_form, values, cosine_table, precision=highest)  21.5 us
    slice x30, local copies, waits for them, and re-layouts, body(): jnp.roll(a, extent - 1, axis=-1)  19.4 us
    slice x30, local copies, waits for them, and re-layouts, body(): jnp.roll(a, -1, axis=-1)  19.2 us
  transfers between devices with their start and end apart: 6, of which 4 were waited for; matrix products, arithmetic and copies ran while one was open for 4% of the time, Pallas kernels for 0%

commit v1 on v0

--- a/solution.py
+++ b/solution.py
@@ -236,7 +236,10 @@
     planes = plane_step(planes, "yzc,kz->ykc", cosine_table, sine_table, 1.0, pair_count)
     planes = plane_step(planes, "yzc,ky->kzc", cosine_table, sine_table, 1.0, pair_count)
     planes = jnp.roll(planes.reshape(plane_size, -1), storage_offset, axis=0)
-    returned = lax.all_to_all(planes, "space", split_axis=0, concat_axis=1, tiled=True)
+    peers = lax.axis_size("space")
+    blocks = jnp.stack(jnp.split(planes, peers, axis=0), axis=0)
+    blocks = lax.all_to_all(blocks, "space", split_axis=0, concat_axis=0)
+    returned = jnp.concatenate(blocks, axis=1)
     returned = returned.reshape(rows_dev, 4, extent, 2, slices)
     real_back = returned[:, :, :, 0]
     imag_back = returned[:, :, :, 1]

time: 415 us -> 468 us (1.13)
  local copies, waits for them, and re-layouts: 116 us -> 168 us
    unnamed x256 -> x355, local copies, waits for them, and re-layouts: 9.81 us -> 58.5 us
where the time goes in v1:
time: 468 us; the launch traced here: 461 us
  local copies, waits for them, and re-layouts  168 us (36%)
  waiting for transfers between devices  90.1 us (19%)
  other arithmetic  68.1 us (15%)
  matrix products  68.1 us (15%)
  blocking collectives  40.9 us (9%)
  starting transfers between devices  15.4 us (3%)
  between operations  9.95 us (2%)
    unnamed x355, local copies, waits for them, and re-layouts  58.5 us
    ppermute x4, waiting for transfers between devices, from_behind(): return lax.ppermute(block, axis, route)  41.5 us
    psum x1, blocking collectives, body(): theta_total = lax.psum(theta_part, ('tm', 'space'))  40.9 us
    dot_general x4, matrix products, plane_step(): with_sin = jnp.einsum(einsum_form, values, sine_table, precision=highest)  27 us
    all_to_all x1, waiting for transfers between devices, body(): blocks = lax.all_to_all(blocks, 'space', split_axis=0, concat_axis=0)  25.8 us
    all_to_all x1, waiting for transfers between devices, body(): lax.all_to_all(packed, 'space', split_axis=1, concat_axis=0, tiled=True)  22.8 us
    dot_general x4, matrix products, plane_step(): with_cos = jnp.einsum(einsum_form, values, cosine_table, precision=highest)  21.6 us
    slice x30, local copies, waits for them, and re-layouts, body(): jnp.roll(a, extent - 1, axis=-1)  19.3 us
  transfers between devices with their start and end apart: 6, of which 4 were waited for; matrix products, arithmetic and copies ran while one was open for 4% of the time, Pallas kernels for 0%

profile of v1, /device:TPU:12, one launch (start us, length us, event | category | flops | bytes accessed | tf_op | source)
XLA Modules:
  0.0 460.7 jit_solution(1600749404201885609)
XLA Ops:
  0.6 3.5 fusion.980
  12.1 16.0 %collective-permute-done = f32[8,2,3,2,2352]{4,0,3,2,1:T(8,128)} collective-permute-done((f32[8,2,3,2,2352]{4,0,3,2,1:T(8,128)}, f32[8,2,3,2,2352]{4,0,3,2,1:T(8,128)}, u32[]{:S(2)}, u32[]{:S(2)}) %collective-permute-start) | collective-permute-done | bytes 903200 | tf_op jit(solution)/shard_map/ppermute | solution.py:17
  40.9 3.7 reshape_reshape.12
  44.6 4.7 %fusion.9 = f32[48,4,8,72]{3,0,2,1:T(8,128)S(1)} fusion(f32[4,2,8,72,48]{4,3,2,1,0:T(8,128)} %reshape_reshape.12), kind=kOutput, calls=%fused_computation.66 | convolution fusion | flops 63721728 | bytes 1622016 | tf_op jit(solution)/shard_map/csqx,kx->qcks/dot_general | solution.py:214
  49.4 4.6 fusion.8
  54.0 3.3 fusion.2
  57.3 3.3 fusion.3
  62.4 2.9 copy.342
  65.3 6.9 %all-to-all-start = ((f32[72,32,96]{2,0,1:T(8,128)}), f32[72,32,96]{2,0,1:T(8,128)}, u32[]{:S(2)}, u32[]{:S(2)}) async-start(f32[72,32,96]{2,0,1:T(8,128)} %copy.342), calls=%async_computation | async-start | bytes 2359296 | tf_op jit(solution)/shard_map/all_to_all | solution.py:217
  74.1 2.8 copy.356
  76.9 22.8 %all-to-all-done = f32[72,32,96]{2,0,1:T(8,128)} async-done(((f32[72,32,96]{2,0,1:T(8,128)}), f32[72,32,96]{2,0,1:T(8,128)}, u32[]{:S(2)}, u32[]{:S(2)}) %all-to-all-start) | async-done | bytes 884768 | tf_op jit(solution)/shard_map/all_to_all | solution.py:217
  101.9 2.3 convolution_bitcast_fusion.2
  104.2 2.3 convolution_bitcast_fusion.3
  106.5 2.9 copy.444
  109.3 2.9 copy.442
  112.3 2.6 fusion.7
  116.5 3.1 copy.351
  119.6 10.3 %fusion.729 = f32[48,48,6,2,8]{1,0,4,3,2:T(8,128)S(1)} fusion(f32[48,6,2,8,48]{4,0,3,2,1:T(8,128)} %bitcast.4520), kind=kOutput, calls=%fused_computation.1675 | convolution fusion | flops 127422720 | bytes 1769472 | tf_op jit(solution)/shard_map/yzc,ky->kzc/dot_general | solution.py:154
  129.9 8.5 %fusion.739 = f32[48,48,6,2,8]{1,0,4,3,2:T(8,128)S(1)} fusion(f32[48,6,2,8,48]{4,0,3,2,1:T(8,128)S(1)} %bitcast.4521), kind=kOutput, calls=%fused_computation.1685 | convolution fusion | flops 127422720 | bytes 1769472 | tf_op jit(solution)/shard_map/yzc,ky->kzc/dot_general | solution.py:153
  140.3 3.2 copy.355
  143.6 4.1 convolution_bitcast_fusion
  147.6 2.3 convolution_bitcast_fusion.1
  149.9 2.8 copy.360
  152.8 2.9 copy.358
  155.7 2.6 slice_subtract_fusion.1
  159.9 3.3 copy.361
  163.2 10.3 %fusion.727 = f32[48,48,6,2,8]{1,0,4,3,2:T(8,128)S(1)} fusion(f32[48,6,2,8,48]{4,0,3,2,1:T(8,128)} %bitcast.4522), kind=kOutput, calls=%fused_computation.1673 | convolution fusion | flops 127422720 | bytes 1769472 | tf_op jit(solution)/shard_map/yzc,ky->kzc/dot_general | solution.py:154
  173.5 8.5 %fusion.741 = f32[48,48,6,2,8]{1,0,4,3,2:T(8,128)S(1)} fusion(f32[48,6,2,8,48]{4,0,3,2,1:T(8,128)S(1)} %bitcast.4523), kind=kOutput, calls=%fused_computation.1687 | convolution fusion | flops 127422720 | bytes 1769472 | tf_op jit(solution)/shard_map/yzc,ky->kzc/dot_general | solution.py:153
  183.9 2.6 reshape_reshape.14
  242.9 5.0 %all-to-all-start.1 = ((f32[32,72,96]{2,1,0:T(8,128)}), f32[32,72,96]{2,1,0:T(8,128)}, u32[]{:S(2)}, u32[]{:S(2)}) async-start(f32[32,72,96]{2,1,0:T(8,128)} %constant_dynamic-update-slice_fusion), calls=%async_computation.1 | async-start | bytes 2359296 | tf_op jit(solution)/shard_map/all_to_all | solution.py:241
  249.8 25.8 %all-to-all-done.1 = f32[32,72,96]{2,1,0:T(8,128)} async-done(((f32[32,72,96]{2,1,0:T(8,128)}), f32[32,72,96]{2,1,0:T(8,128)}, u32[]{:S(2)}, u32[]{:S(2)}) %all-to-all-start.1) | async-done | bytes 884768 | tf_op jit(solution)/shard_map/all_to_all | solution.py:241
  275.6 2.9 copy.397
  285.0 2.9 copy.400
  287.9 2.3 reshape.11985
  303.4 2.6 collective-permute-start.3
  309.8 25.6 %collective-permute-done.2 = f32[3,3,2,8,2256]{4,3,2,1,0:T(8,128)} collective-permute-done((f32[3,3,2,8,2256]{4,3,2,1,0:T(8,128)S(1)}, f32[3,3,2,8,2256]{4,3,2,1,0:T(8,128)}, u32[]{:S(2)}, u32[]{:S(2)}) %collective-permute-start.2) | collective-permute-done | bytes 1299488 | tf_op jit(solution)/shard_map/ppermute | solution.py:17
  335.3 6.6 %concatenate.1157 = f32[3,3,2,8,8016]{4,3,2,1,0:T(8,128)} concatenate(f32[3,3,2,8,2256]{4,3,2,1,0:T(8,128)} %collective-permute-done.2, f32[3,3,2,8,3456]{4,3,2,1,0:T(8,128)} %copy-done.7, f32[3,3,2,8,2304]{4,3,2,1,0:T(8,128)} %collective-permute-done.3), dimensions={4} | concatenate | bytes 9234432 | tf_op jit(solution)/shard_map/concatenate | solution.py:259
  342.1 2.9 slice_bitcast_fusion.17
  345.2 2.9 fusion.706
  380.0 2.8 fusion.707
  392.7 2.5 fusion.170
  395.8 2.5 fusion.177
  398.9 2.6 fusion.95
  402.0 2.5 fusion.102
  406.0 2.7 pad_maximum_fusion
  409.2 3.4 fusion.708
  413.2 4.0 copy.419
  417.2 40.9 %all-reduce = (f32[]{:T(128)}, f32[8]{0:T(128)S(1)}) all-reduce(f32[]{:T(128)S(6)} %add.9190, f32[8]{0:T(128)S(1)} %add_add_fusion.11), channel_id=1, replica_groups=mesh['tm'=1,'space'=32] {'tm','space'}, use_global_device_ids=true, to_apply=%region_8.9 | all-reduce | flops 9 | bytes 72 | tf_op jit(solution)/shard_map/psum | solution.py:198
  (544 shorter events, 155.5 us)
Async XLA Ops:
  5.2 24.8 %collective-permute-start.1 = (f32[8,2,3,2,2256]{4,0,3,2,1:T(8,128)}, f32[8,2,3,2,2256]{4,0,3,2,1:T(8,128)}, u32[]{:S(2)}, u32[]{:S(2)}) collective-permute-start(f32[8,2,3,2,2256]{4,0,3,2,1:T(8,128)} %slice.1148), channel_id=1, source_target_pairs={{1,0},{2,1},{3,2},{4,3},{5,4},{6,5},{7,6},{8,7},{9,8},{10,9},{11,1... | collective-permute-start | bytes 2598920 | tf_op jit(solution)/shard_map/ppermute | solution.py:17
  7.5 20.5 %collective-permute-start = (f32[8,2,3,2,2352]{4,0,3,2,1:T(8,128)}, f32[8,2,3,2,2352]{4,0,3,2,1:T(8,128)}, u32[]{:S(2)}, u32[]{:S(2)}) collective-permute-start(f32[8,2,3,2,2352]{4,0,3,2,1:T(8,128)} %pad_maximum_fusion.9), channel_id=1, source_target_pairs={{31,0},{0,1},{1,2},{2,3},{3,4},{4,5},{5,6},{6,7},{7,8},{8,9},{9,10... | collective-permute-start | bytes 2709512 | tf_op jit(solution)/shard_map/ppermute | solution.py:17
  12.0 27.8 %copy-start = (f32[8,2,3,2,3456]{4,0,3,2,1:T(8,128)}, f32[8,2,3,2,3456]{4,0,3,2,1:T(8,128)S(1)}, u32[]{:S(2)}) copy-start(f32[8,2,3,2,3456]{4,0,3,2,1:T(8,128)S(1)} %maximum_select_fusion) | copy-start | bytes 3981316
  12.0 18.0 %copy-start.91 = (f32[8,2,3,2,1200]{4,0,3,2,1:T(8,128)S(1)}, f32[8,2,3,2,1200]{4,0,3,2,1:T(8,128)}, u32[]{:S(2)}) copy-start(f32[8,2,3,2,1200]{4,0,3,2,1:T(8,128)} %slice.1147) | copy-start | bytes 1382404
  32.0 7.8 %copy-start.2 = (f32[8,2,3,2,3456]{4,0,3,2,1:T(8,128)}, f32[8,2,3,2,3456]{4,0,3,2,1:T(8,128)S(1)}, u32[]{:S(2)}) copy-start(f32[8,2,3,2,3456]{4,0,3,2,1:T(8,128)S(1)} %maximum_select_fusion.1) | copy-start | bytes 3981316
  32.9 7.0 %copy-start.17 = (f32[8,1,1,1,3456]{4,0,3,2,1:T(8,128)}, f32[8,1,1,1,3456]{4,0,3,2,1:T(8,128)S(1)}, u32[]{:S(2)}) copy-start(f32[8,1,1,1,3456]{4,0,3,2,1:T(8,128)S(1)} %get-tuple-element.93) | copy-start | bytes 331780
  44.6 9.3 %copy-start.10 = (f32[4,2,8,72,48]{4,3,2,1,0:T(8,128)S(1)}, f32[4,2,8,72,48]{4,3,2,1,0:T(8,128)}, u32[]{:S(2)}) copy-start(f32[4,2,8,72,48]{4,3,2,1,0:T(8,128)} %reshape_reshape.12) | copy-start | bytes 2654212
  65.3 34.4 %all-to-all-start = ((f32[72,32,96]{2,0,1:T(8,128)}), f32[72,32,96]{2,0,1:T(8,128)}, u32[]{:S(2)}, u32[]{:S(2)}) async-start(f32[72,32,96]{2,0,1:T(8,128)} %copy.342), calls=%async_computation | async-start | bytes 2359296 | tf_op jit(solution)/shard_map/all_to_all | solution.py:217
  119.6 10.3 %copy-start.8 = (f32[48,48,96]{0,1,2:T(8,128)S(1)}, f32[48,48,96]{0,1,2:T(8,128)}, u32[]{:S(2)}) copy-start(f32[48,48,96]{0,1,2:T(8,128)} %copy.351) | copy-start | bytes 2654212
  163.2 10.3 %copy-start.9 = (f32[48,96,48]{2,0,1:T(8,128)S(1)}, f32[48,96,48]{2,0,1:T(8,128)}, u32[]{:S(2)}) copy-start(f32[48,96,48]{2,0,1:T(8,128)} %copy.361) | copy-start | bytes 2654212
  190.9 22.4 %copy-start.139 = (f32[72,96]{0,1:T(8,128)S(1)}, f32[72,96]{0,1:T(8,128)}, u32[]{:S(2)}) copy-start(f32[72,96]{0,1:T(8,128)} %get-tuple-element.311) | copy-start | bytes 82948
  190.9 22.4 %copy-start.138 = (f32[72,96]{0,1:T(8,128)S(1)}, f32[72,96]{0,1:T(8,128)}, u32[]{:S(2)}) copy-start(f32[72,96]{0,1:T(8,128)} %get-tuple-element.310) | copy-start | bytes 82948
  190.9 22.5 %copy-start.137 = (f32[72,96]{0,1:T(8,128)S(1)}, f32[72,96]{0,1:T(8,128)}, u32[]{:S(2)}) copy-start(f32[72,96]{0,1:T(8,128)} %get-tuple-element.309) | copy-start | bytes 82948
  190.9 22.6 %copy-start.136 = (f32[72,96]{0,1:T(8,128)S(1)}, f32[72,96]{0,1:T(8,128)}, u32[]{:S(2)}) copy-start(f32[72,96]{0,1:T(8,128)} %get-tuple-element.308) | copy-start | bytes 82948
  190.9 22.7 %copy-start.135 = (f32[72,96]{0,1:T(8,128)S(1)}, f32[72,96]{0,1:T(8,128)}, u32[]{:S(2)}) copy-start(f32[72,96]{0,1:T(8,128)} %get-tuple-element.307) | copy-start | bytes 82948
  190.9 22.8 %copy-start.134 = (f32[72,96]{0,1:T(8,128)S(1)}, f32[72,96]{0,1:T(8,128)}, u32[]{:S(2)}) copy-start(f32[72,96]{0,1:T(8,128)} %get-tuple-element.306) | copy-start | bytes 82948
  191.0 22.9 %copy-start.133 = (f32[72,96]{0,1:T(8,128)S(1)}, f32[72,96]{0,1:T(8,128)}, u32[]{:S(2)}) copy-start(f32[72,96]{0,1:T(8,128)} %get-tuple-element.305) | copy-start | bytes 82948
  191.0 22.9 %copy-start.132 = (f32[72,96]{0,1:T(8,128)S(1)}, f32[72,96]{0,1:T(8,128)}, u32[]{:S(2)}) copy-start(f32[72,96]{0,1:T(8,128)} %get-tuple-element.304) | copy-start | bytes 82948
  191.0 23.0 %copy-start.131 = (f32[72,96]{0,1:T(8,128)S(1)}, f32[72,96]{0,1:T(8,128)}, u32[]{:S(2)}) copy-start(f32[72,96]{0,1:T(8,128)} %get-tuple-element.303) | copy-start | bytes 82948
  191.0 23.1 %copy-start.130 = (f32[72,96]{0,1:T(8,128)S(1)}, f32[72,96]{0,1:T(8,128)}, u32[]{:S(2)}) copy-start(f32[72,96]{0,1:T(8,128)} %get-tuple-element.302) | copy-start | bytes 82948
  191.0 23.2 %copy-start.129 = (f32[72,96]{0,1:T(8,128)S(1)}, f32[72,96]{0,1:T(8,128)}, u32[]{:S(2)}) copy-start(f32[72,96]{0,1:T(8,128)} %get-tuple-element.301) | copy-start | bytes 82948
  191.0 23.3 %copy-start.128 = (f32[72,96]{0,1:T(8,128)S(1)}, f32[72,96]{0,1:T(8,128)}, u32[]{:S(2)}) copy-start(f32[72,96]{0,1:T(8,128)} %get-tuple-element.300) | copy-start | bytes 82948
  191.0 23.3 %copy-start.127 = (f32[72,96]{0,1:T(8,128)S(1)}, f32[72,96]{0,1:T(8,128)}, u32[]{:S(2)}) copy-start(f32[72,96]{0,1:T(8,128)} %get-tuple-element.299) | copy-start | bytes 82948
  191.0 23.4 %copy-start.126 = (f32[72,96]{0,1:T(8,128)S(1)}, f32[72,96]{0,1:T(8,128)}, u32[]{:S(2)}) copy-start(f32[72,96]{0,1:T(8,128)} %get-tuple-element.298) | copy-start | bytes 82948
  191.0 23.5 %copy-start.125 = (f32[72,96]{0,1:T(8,128)S(1)}, f32[72,96]{0,1:T(8,128)}, u32[]{:S(2)}) copy-start(f32[72,96]{0,1:T(8,128)} %get-tuple-element.297) | copy-start | bytes 82948
  192.1 22.6 %copy-start.124 = (f32[72,96]{0,1:T(8,128)S(1)}, f32[72,96]{0,1:T(8,128)}, u32[]{:S(2)}) copy-start(f32[72,96]{0,1:T(8,128)} %get-tuple-element.296) | copy-start | bytes 82948
  242.9 32.8 %all-to-all-start.1 = ((f32[32,72,96]{2,1,0:T(8,128)}), f32[32,72,96]{2,1,0:T(8,128)}, u32[]{:S(2)}, u32[]{:S(2)}) async-start(f32[32,72,96]{2,1,0:T(8,128)} %constant_dynamic-update-slice_fusion), calls=%async_computation.1 | async-start | bytes 2359296 | tf_op jit(solution)/shard_map/all_to_all | solution.py:241
  294.4 14.3 %copy-start.29 = (f32[8,3456]{1,0:T(8,128)}, f32[8,3456]{1,0:T(8,128)S(1)}, u32[]{:S(2)}) copy-start(f32[8,3456]{1,0:T(8,128)S(1)} %get-tuple-element.199) | copy-start | bytes 331780
  294.4 14.3 %copy-start.32 = (f32[8,3456]{1,0:T(8,128)}, f32[8,3456]{1,0:T(8,128)S(1)}, u32[]{:S(2)}) copy-start(f32[8,3456]{1,0:T(8,128)S(1)} %get-tuple-element.200) | copy-start | bytes 331780
  294.4 14.3 %copy-start.35 = (f32[8,3456]{1,0:T(8,128)}, f32[8,3456]{1,0:T(8,128)S(1)}, u32[]{:S(2)}) copy-start(f32[8,3456]{1,0:T(8,128)S(1)} %get-tuple-element.201) | copy-start | bytes 331780
  294.4 14.3 %copy-start.38 = (f32[8,3456]{1,0:T(8,128)}, f32[8,3456]{1,0:T(8,128)S(1)}, u32[]{:S(2)}) copy-start(f32[8,3456]{1,0:T(8,128)S(1)} %get-tuple-element.203) | copy-start | bytes 331780
  294.4 14.3 %copy-start.41 = (f32[8,3456]{1,0:T(8,128)}, f32[8,3456]{1,0:T(8,128)S(1)}, u32[]{:S(2)}) copy-start(f32[8,3456]{1,0:T(8,128)S(1)} %get-tuple-element.205) | copy-start | bytes 331780
  294.4 14.3 %copy-start.44 = (f32[8,3456]{1,0:T(8,128)}, f32[8,3456]{1,0:T(8,128)S(1)}, u32[]{:S(2)}) copy-start(f32[8,3456]{1,0:T(8,128)S(1)} %get-tuple-element.208) | copy-start | bytes 331780
  303.4 32.0 %collective-permute-start.2 = (f32[3,3,2,8,2256]{4,3,2,1,0:T(8,128)S(1)}, f32[3,3,2,8,2256]{4,3,2,1,0:T(8,128)}, u32[]{:S(2)}, u32[]{:S(2)}) collective-permute-start(f32[3,3,2,8,2256]{4,3,2,1,0:T(8,128)S(1)} %slice.1332), channel_id=1, source_target_pairs={{31,0},{0,1},{1,2},{2,3},{3,4},{4,5},{5,6},{6,7},{7,8},{8,9},{9,10... | collective-permute-start | bytes 3898376 | tf_op jit(solution)/shard_map/ppermute | solution.py:17
  303.4 31.9 %collective-permute-start.3 = (f32[3,3,2,8,2304]{4,3,2,1,0:T(8,128)S(1)}, f32[3,3,2,8,2304]{4,3,2,1,0:T(8,128)}, u32[]{:S(2)}, u32[]{:S(2)}) collective-permute-start(f32[3,3,2,8,2304]{4,3,2,1,0:T(8,128)S(1)} %slice.1333), channel_id=1, source_target_pairs={{1,0},{2,1},{3,2},{4,3},{5,4},{6,5},{7,6},{8,7},{9,8},{10,9},{11,1... | collective-permute-start | bytes 3981320 | tf_op jit(solution)/shard_map/ppermute | solution.py:17
  348.1 31.8 %copy-start.69 = (f32[8,3456]{1,0:T(8,128)}, f32[8,3456]{1,0:T(8,128)S(1)}, u32[]{:S(2)}) copy-start(f32[8,3456]{1,0:T(8,128)S(1)} %get-tuple-element.21) | copy-start | bytes 331780
  348.1 31.8 %copy-start.71 = (f32[8,3456]{1,0:T(8,128)}, f32[8,3456]{1,0:T(8,128)S(1)}, u32[]{:S(2)}) copy-start(f32[8,3456]{1,0:T(8,128)S(1)} %get-tuple-element.22) | copy-start | bytes 331780
  348.1 31.8 %copy-start.73 = (f32[8,3456]{1,0:T(8,128)}, f32[8,3456]{1,0:T(8,128)S(1)}, u32[]{:S(2)}) copy-start(f32[8,3456]{1,0:T(8,128)S(1)} %get-tuple-element.23) | copy-start | bytes 331780
  348.1 31.8 %copy-start.75 = (f32[8,3456]{1,0:T(8,128)}, f32[8,3456]{1,0:T(8,128)S(1)}, u32[]{:S(2)}) copy-start(f32[8,3456]{1,0:T(8,128)S(1)} %get-tuple-element.24) | copy-start | bytes 331780
  348.1 31.8 %copy-start.77 = (f32[8,3456]{1,0:T(8,128)}, f32[8,3456]{1,0:T(8,128)S(1)}, u32[]{:S(2)}) copy-start(f32[8,3456]{1,0:T(8,128)S(1)} %get-tuple-element.26) | copy-start | bytes 331780
  348.1 31.8 %copy-start.79 = (f32[8,3456]{1,0:T(8,128)}, f32[8,3456]{1,0:T(8,128)S(1)}, u32[]{:S(2)}) copy-start(f32[8,3456]{1,0:T(8,128)S(1)} %get-tuple-element.44) | copy-start | bytes 331780
  348.1 31.8 %copy-start.81 = (f32[8,3456]{1,0:T(8,128)}, f32[8,3456]{1,0:T(8,128)S(1)}, u32[]{:S(2)}) copy-start(f32[8,3456]{1,0:T(8,128)S(1)} %get-tuple-element.45) | copy-start | bytes 331780
  348.2 31.8 %copy-start.83 = (f32[8,3456]{1,0:T(8,128)}, f32[8,3456]{1,0:T(8,128)S(1)}, u32[]{:S(2)}) copy-start(f32[8,3456]{1,0:T(8,128)S(1)} %get-tuple-element.46) | copy-start | bytes 331780
  348.2 31.8 %copy-start.85 = (f32[8,3456]{1,0:T(8,128)}, f32[8,3456]{1,0:T(8,128)S(1)}, u32[]{:S(2)}) copy-start(f32[8,3456]{1,0:T(8,128)S(1)} %get-tuple-element.47) | copy-start | bytes 331780
  348.2 31.8 %copy-start.87 = (f32[8,3456]{1,0:T(8,128)}, f32[8,3456]{1,0:T(8,128)S(1)}, u32[]{:S(2)}) copy-start(f32[8,3456]{1,0:T(8,128)S(1)} %get-tuple-element.48) | copy-start | bytes 331780
  348.2 31.8 %copy-start.89 = (f32[8,3456]{1,0:T(8,128)}, f32[8,3456]{1,0:T(8,128)S(1)}, u32[]{:S(2)}) copy-start(f32[8,3456]{1,0:T(8,128)S(1)} %get-tuple-element.49) | copy-start | bytes 331780
  348.2 31.8 %copy-start.92 = (f32[8,3456]{1,0:T(8,128)}, f32[8,3456]{1,0:T(8,128)S(1)}, u32[]{:S(2)}) copy-start(f32[8,3456]{1,0:T(8,128)S(1)} %get-tuple-element.25) | copy-start | bytes 331780
  369.9 10.1 %copy-start.143 = (pred[3456]{0:T(1024)(128)(4,1)S(1)}, pred[3456]{0:T(1024)(128)(4,1)}, u32[]{:S(2)}) copy-start(pred[3456]{0:T(1024)(128)(4,1)} %broadcast_compare_fusion) | copy-start | bytes 10372
  (102 other events, 286.4 us)
